TPU v7x, 32 devices: a whole 2x2x4 slice. The times are simulated.
32 devices in a mesh: row: 16 (over z, x, core), feat: 2 (over y).
Axes of the slice: x: 2, y: 2, z: 4, core: 2. Of those that a mesh axis runs over, the one named last changes fastest.
Arguments:
- bin_index: int32 [1024, 49152], P('feat', 'row'), may hold values from 0 to 63
- gradient: bfloat16 [32, 49152], P(None, ('row', 'feat')), may hold values from -6 to 6
- hessian: bfloat16 [49152], P(('row', 'feat')), may hold values from 0.25 to 4
- row_node: int32 [49152], P('row'), may hold values from 0 to 7
Outputs:
- split_gain: float32 [1024, 512], P(('feat', 'row'))
- best_gain: float32 [8], replicated
All inputs are finite; a program needn't handle non-finite values.
Results may differ from a plain program's by a relative error of at most 0.0003.
Values may be sent and summed in bfloat16 or wider, within the bound.
A program may use at most 128 MiB of HBM per device.

v0:
```python
import math

import jax
import jax.numpy as jnp
from jax import lax
from jax.sharding import PartitionSpec as P

BINS = 64
NODES = 8


ridge_term = 1.0


def masked_rows(node_ids, grad_rows, hess_rows):
    stacked = jnp.concatenate([grad_rows, hess_rows[None, :]], 0)
    picked = (node_ids[None, :] == jnp.arange(NODES, dtype=jnp.int32)[:, None]).astype(jnp.bfloat16)
    return (picked[:, None, :] * stacked[None, :, :]).reshape(-1, node_ids.shape[0])


def histogram_block(feature_block, masked):
    levels = jnp.arange(BINS, dtype=jnp.int32)
    onehot = (feature_block[:, None, :] == levels[None, :, None]).astype(jnp.bfloat16)
    return jnp.einsum("fbr,mr->fbm", onehot, masked, preferred_element_type=jnp.float32)


def score_splits(histogram, node_totals):
    left_sums = jnp.cumsum(histogram, axis=1)
    whole_sums = node_totals[None, None]
    right_sums = whole_sums - left_sums

    def part_score(sums):
        return jnp.sum(sums[..., :-1] * sums[..., :-1], axis=-1) / (sums[..., -1] + ridge_term)

    outputs_count = histogram.shape[-1] - 1
    score_terms = part_score(left_sums) + part_score(right_sums) - part_score(whole_sums)
    return jnp.transpose(0.5 / outputs_count * score_terms, (0, 2, 1))


def on_device(bin_index, gradient, hessian, row_node):
    local_features = bin_index.shape[0]
    owned_count = local_features // lax.axis_size("row")
    outputs_count = gradient.shape[0]
    shard_rows = gradient.shape[1]
    first_local = lax.axis_index("feat") * shard_rows
    local_nodes = lax.dynamic_slice_in_dim(row_node, first_local, shard_rows, 0)
    stacked = jnp.concatenate([gradient, hessian[None, :]], 0)
    picked = (local_nodes[None, :] == jnp.arange(NODES, dtype=jnp.int32)[:, None]).astype(
        jnp.bfloat16
    )
    local_totals = jnp.einsum("nr,mr->nm", picked, stacked, preferred_element_type=jnp.float32)
    node_totals = lax.psum(local_totals, ("row", "feat"))
    columns = lax.all_to_all(bin_index, "row", split_axis=0, concat_axis=1, tiled=True)
    grad_rows, hess_rows = (
        lax.all_gather(gradient, ("row", "feat"), axis=1, tiled=True),
        lax.all_gather(hessian, ("row", "feat"), axis=0, tiled=True),
    )
    node_rows = lax.all_gather(row_node, "row", axis=0, tiled=True)
    total_rows = columns.shape[1]
    row_span = math.gcd(total_rows, 4096)

    def add_block(step_index, running):
        lower = step_index * row_span
        feature_block = lax.dynamic_slice_in_dim(columns, lower, row_span, 1)
        grad_block = lax.dynamic_slice_in_dim(grad_rows, lower, row_span, 1)
        hess_block = lax.dynamic_slice_in_dim(hess_rows, lower, row_span, 0)
        node_block = lax.dynamic_slice_in_dim(node_rows, lower, row_span, 0)
        return running + histogram_block(
            feature_block, masked_rows(node_block, grad_block, hess_block)
        )

    zeros = jnp.zeros((owned_count, BINS, NODES * (outputs_count + 1)), jnp.float32)
    owned = lax.fori_loop(0, total_rows // row_span, add_block, zeros).reshape(owned_count, -1)
    histogram = owned.reshape(owned_count, BINS, NODES, outputs_count + 1)
    split_gain = score_splits(histogram, node_totals)
    best_gain = lax.pmax(jnp.max(split_gain, axis=(0, 2)), ("row", "feat"))
    return (split_gain.reshape(owned_count, NODES * BINS), best_gain)


def solution(mesh):
    in_specs = (P("feat", "row"), P(None, ("row", "feat")), P(("row", "feat")), P("row"))
    out_specs = (P(("feat", "row"), None), P())
    return jax.shard_map(
        on_device, mesh=mesh, in_specs=in_specs, out_specs=out_specs, check_vma=False
    )
```

profile of v0, /device:TPU:12, one launch (start us, length us, event | category | flops | bytes accessed | tf_op | source)
XLA Modules:
  0.0 568.1 jit_solution(2930947856876455961)
XLA Ops:
  7.2 6.4 %all-to-all-start = ((s32[16,32,3072]{2,1,0:T(8,128)}), s32[16,32,3072]{2,1,0:T(8,128)}, u32[]{:S(2)}, u32[]{:S(2)}) async-start(s32[16,32,3072]{2,1,0:T(8,128)} %bitcast.31), calls=%async_computation | async-start | bytes 12582912 | tf_op jit(solution)/shard_map/all_to_all | solution.py:53
  14.4 192.8 %all-gather = bf16[32,1,1536]{2,1,0:T(2,128)(2,1)S(1)} all-gather(bf16[1,1,1536]{2,1,0:T(2,128)(2,1)S(1)} %reshape.61), channel_id=1, replica_groups=mesh['row'=16,'feat'=2] {'row','feat'}, dimensions={0}, use_global_device_ids=true | all-gather | bytes 101376 | tf_op jit(solution)/shard_map/all_gather | solution.py:56
  208.1 43.6 %psum.7 = f32[8,33]{1,0:T(8,128)S(1)} all-reduce(f32[8,33]{1,0:T(8,128)S(1)} %fusion.12), channel_id=1, replica_groups=mesh['row'=16,'feat'=2] {'row','feat'}, use_global_device_ids=true, to_apply=%region_4.5 | all-reduce | flops 264 | bytes 2112 | tf_op jit(solution)/shard_map/psum | solution.py:52
  252.1 19.0 %all_gather.9 = s32[49152]{0:T(1024)S(1)} all-gather(s32[3072]{0:T(1024)S(1)} %copy-done.3), channel_id=1, replica_groups=mesh['row'=16,'feat'=2] {'row'}, dimensions={0}, use_global_device_ids=true | all-gather | bytes 208896 | tf_op jit(solution)/shard_map/all_gather | solution.py:58
  271.1 6.2 %copy.45 = s32[16,4,8,3072]{3,2,0,1:T(8,128)} copy(s32[16,4,8,3072]{3,2,1,0:T(8,128)} %bitcast.7) | data formatting | bytes 12582912 | tf_op jit(solution)/shard_map/all_to_all | solution.py:53
  277.3 201.6 %while.14 = (s32[]{:T(128)}, f32[32,64,264]{2,1,0:T(8,128)}, s32[32,49152]{1,0:T(8,128)}, s32[49152]{0:T(1024)S(1)}, bf16[32,49152]{1,0:T(8,128)(2,1)}, /*index=...) while((s32[]{:T(128)}, f32[32,64,264]{2,1,0:T(8,128)}, ...), condition=%wide.region_1.0_spmd.clone, body=%wide.region_0.0_spmd.clone.sunk | while | flops 4440342528 | bytes 16097461 | solution.py:73
  281.8 11.9 %select_add_fusion.2 = f32[32,64,264]{2,1,0:T(8,128)} fusion(f32[32,64,264]{2,1,0:T(8,128)} %get-tuple-element.195, bf16[264,4096,1]{1,0,2:T(8,128)(2,1)} %reshape.68, s32[32,4096]{1,0:T(8,128)S(1)} %constant_dynamic-slice_fusion.5, pred[]{:T(512)S(6)} %compare.3), kind=kOutput, calls=%fused_computation.3.clone.1 | convolution fusion | flops 4438654976 | bytes 7012353 | tf_op jit(solution)/shard_map/while/body/eval_jaxpr/fbr,mr->fbm/dot_general | solution.py:24
  298.1 12.4 %select_add_fusion.2 = f32[32,64,264]{2,1,0:T(8,128)} fusion(f32[32,64,264]{2,1,0:T(8,128)} %get-tuple-element.195, bf16[264,4096,1]{1,0,2:T(8,128)(2,1)} %reshape.68, s32[32,4096]{1,0:T(8,128)S(1)} %constant_dynamic-slice_fusion.5, pred[]{:T(512)S(6)} %compare.3), kind=kOutput, calls=%fused_computation.3.clone.1 | convolution fusion | flops 4438654976 | bytes 7012353 | tf_op jit(solution)/shard_map/while/body/eval_jaxpr/fbr,mr->fbm/dot_general | solution.py:24
  315.0 12.4 %select_add_fusion.2 = f32[32,64,264]{2,1,0:T(8,128)} fusion(f32[32,64,264]{2,1,0:T(8,128)} %get-tuple-element.195, bf16[264,4096,1]{1,0,2:T(8,128)(2,1)} %reshape.68, s32[32,4096]{1,0:T(8,128)S(1)} %constant_dynamic-slice_fusion.5, pred[]{:T(512)S(6)} %compare.3), kind=kOutput, calls=%fused_computation.3.clone.1 | convolution fusion | flops 4438654976 | bytes 7012353 | tf_op jit(solution)/shard_map/while/body/eval_jaxpr/fbr,mr->fbm/dot_general | solution.py:24
  331.8 12.4 %select_add_fusion.2 = f32[32,64,264]{2,1,0:T(8,128)} fusion(f32[32,64,264]{2,1,0:T(8,128)} %get-tuple-element.195, bf16[264,4096,1]{1,0,2:T(8,128)(2,1)} %reshape.68, s32[32,4096]{1,0:T(8,128)S(1)} %constant_dynamic-slice_fusion.5, pred[]{:T(512)S(6)} %compare.3), kind=kOutput, calls=%fused_computation.3.clone.1 | convolution fusion | flops 4438654976 | bytes 7012353 | tf_op jit(solution)/shard_map/while/body/eval_jaxpr/fbr,mr->fbm/dot_general | solution.py:24
  348.7 12.4 %select_add_fusion.2 = f32[32,64,264]{2,1,0:T(8,128)} fusion(f32[32,64,264]{2,1,0:T(8,128)} %get-tuple-element.195, bf16[264,4096,1]{1,0,2:T(8,128)(2,1)} %reshape.68, s32[32,4096]{1,0:T(8,128)S(1)} %constant_dynamic-slice_fusion.5, pred[]{:T(512)S(6)} %compare.3), kind=kOutput, calls=%fused_computation.3.clone.1 | convolution fusion | flops 4438654976 | bytes 7012353 | tf_op jit(solution)/shard_map/while/body/eval_jaxpr/fbr,mr->fbm/dot_general | solution.py:24
  365.5 12.4 %select_add_fusion.2 = f32[32,64,264]{2,1,0:T(8,128)} fusion(f32[32,64,264]{2,1,0:T(8,128)} %get-tuple-element.195, bf16[264,4096,1]{1,0,2:T(8,128)(2,1)} %reshape.68, s32[32,4096]{1,0:T(8,128)S(1)} %constant_dynamic-slice_fusion.5, pred[]{:T(512)S(6)} %compare.3), kind=kOutput, calls=%fused_computation.3.clone.1 | convolution fusion | flops 4438654976 | bytes 7012353 | tf_op jit(solution)/shard_map/while/body/eval_jaxpr/fbr,mr->fbm/dot_general | solution.py:24
  382.4 12.4 %select_add_fusion.2 = f32[32,64,264]{2,1,0:T(8,128)} fusion(f32[32,64,264]{2,1,0:T(8,128)} %get-tuple-element.195, bf16[264,4096,1]{1,0,2:T(8,128)(2,1)} %reshape.68, s32[32,4096]{1,0:T(8,128)S(1)} %constant_dynamic-slice_fusion.5, pred[]{:T(512)S(6)} %compare.3), kind=kOutput, calls=%fused_computation.3.clone.1 | convolution fusion | flops 4438654976 | bytes 7012353 | tf_op jit(solution)/shard_map/while/body/eval_jaxpr/fbr,mr->fbm/dot_general | solution.py:24
  399.2 12.4 %select_add_fusion.2 = f32[32,64,264]{2,1,0:T(8,128)} fusion(f32[32,64,264]{2,1,0:T(8,128)} %get-tuple-element.195, bf16[264,4096,1]{1,0,2:T(8,128)(2,1)} %reshape.68, s32[32,4096]{1,0:T(8,128)S(1)} %constant_dynamic-slice_fusion.5, pred[]{:T(512)S(6)} %compare.3), kind=kOutput, calls=%fused_computation.3.clone.1 | convolution fusion | flops 4438654976 | bytes 7012353 | tf_op jit(solution)/shard_map/while/body/eval_jaxpr/fbr,mr->fbm/dot_general | solution.py:24
  416.0 12.4 %select_add_fusion.2 = f32[32,64,264]{2,1,0:T(8,128)} fusion(f32[32,64,264]{2,1,0:T(8,128)} %get-tuple-element.195, bf16[264,4096,1]{1,0,2:T(8,128)(2,1)} %reshape.68, s32[32,4096]{1,0:T(8,128)S(1)} %constant_dynamic-slice_fusion.5, pred[]{:T(512)S(6)} %compare.3), kind=kOutput, calls=%fused_computation.3.clone.1 | convolution fusion | flops 4438654976 | bytes 7012353 | tf_op jit(solution)/shard_map/while/body/eval_jaxpr/fbr,mr->fbm/dot_general | solution.py:24
  432.9 12.4 %select_add_fusion.2 = f32[32,64,264]{2,1,0:T(8,128)} fusion(f32[32,64,264]{2,1,0:T(8,128)} %get-tuple-element.195, bf16[264,4096,1]{1,0,2:T(8,128)(2,1)} %reshape.68, s32[32,4096]{1,0:T(8,128)S(1)} %constant_dynamic-slice_fusion.5, pred[]{:T(512)S(6)} %compare.3), kind=kOutput, calls=%fused_computation.3.clone.1 | convolution fusion | flops 4438654976 | bytes 7012353 | tf_op jit(solution)/shard_map/while/body/eval_jaxpr/fbr,mr->fbm/dot_general | solution.py:24
  449.7 12.4 %select_add_fusion.2 = f32[32,64,264]{2,1,0:T(8,128)} fusion(f32[32,64,264]{2,1,0:T(8,128)} %get-tuple-element.195, bf16[264,4096,1]{1,0,2:T(8,128)(2,1)} %reshape.68, s32[32,4096]{1,0:T(8,128)S(1)} %constant_dynamic-slice_fusion.5, pred[]{:T(512)S(6)} %compare.3), kind=kOutput, calls=%fused_computation.3.clone.1 | convolution fusion | flops 4438654976 | bytes 7012353 | tf_op jit(solution)/shard_map/while/body/eval_jaxpr/fbr,mr->fbm/dot_general | solution.py:24
  466.6 12.4 %select_add_fusion.2 = f32[32,64,264]{2,1,0:T(8,128)} fusion(f32[32,64,264]{2,1,0:T(8,128)} %get-tuple-element.195, bf16[264,4096,1]{1,0,2:T(8,128)(2,1)} %reshape.68, s32[32,4096]{1,0:T(8,128)S(1)} %constant_dynamic-slice_fusion.5, pred[]{:T(512)S(6)} %compare.3), kind=kOutput, calls=%fused_computation.3.clone.1 | convolution fusion | flops 4438654976 | bytes 7012353 | tf_op jit(solution)/shard_map/while/body/eval_jaxpr/fbr,mr->fbm/dot_general | solution.py:24
  478.9 6.9 %copy.36 = f32[32,64,264]{1,0,2:T(8,128)} copy(f32[32,64,264]{2,1,0:T(8,128)} %get-tuple-element.111) | data formatting | bytes 4325376 | tf_op jit(solution)/shard_map/while | solution.py:73
  485.8 7.1 %copy.37 = f32[32,64,8,33]{3,2,1,0:T(8,128)} copy(f32[32,64,8,33]{1,0,3,2:T(8,128)} %bitcast.29) | data formatting | bytes 4325376 | tf_op jit(solution)/shard_map/reshape;reshape | solution.py:74
  492.9 7.2 %fusion.20 = f32[32,64,8,33]{3,2,1,0:T(8,128)} fusion(f32[32,64,8,33]{3,2,1,0:T(8,128)} %copy.37), kind=kOutput, calls=%fused_computation.34 | output fusion | flops 34062336 | bytes 4325376 | tf_op jit(solution)/shard_map/jit(cumsum)/reduce_window_sum | solution.py:28
  500.0 7.9 %copy.38 = f32[32,64,8,33]{1,2,3,0:T(8,128)} copy(f32[32,64,8,33]{3,2,1,0:T(8,128)} %fusion.20) | data formatting | bytes 4325376 | tf_op jit(solution)/shard_map/jit(cumsum)/reduce_window_sum | solution.py:28
  507.9 5.8 %fusion.3 = f32[32,64,8]{2,1,0:T(8,128)S(1)} fusion(f32[32,64,8,33]{3,2,1,0:T(8,128)} %fusion.20), kind=kLoop, calls=%fused_computation.11 | loop fusion | flops 1032192 | bytes 2162688 | tf_op jit(solution)/shard_map/reduce_sum | solution.py:33
  518.8 42.4 %pmax.7 = f32[8]{0:T(128)} all-reduce(f32[8]{0:T(128)S(1)} %get-tuple-element.145), channel_id=1, replica_groups=mesh['row'=16,'feat'=2] {'row','feat'}, use_global_device_ids=true, to_apply=%region_8.9 | all-reduce | flops 8 | bytes 64 | tf_op jit(solution)/shard_map/pmax | solution.py:76
  (138 shorter events, 60.3 us)
Async XLA Ops:
  7.2 7.2 %copy-start.4 = (bf16[1536]{0:T(1024)(128)(2,1)S(1)}, bf16[1536]{0:T(1024)(128)(2,1)}, u32[]{:S(2)}) copy-start(bf16[1536]{0:T(1024)(128)(2,1)} %param.8) | copy-start | bytes 9220
  7.2 200.7 %copy-start.3 = (s32[3072]{0:T(1024)S(1)}, s32[3072]{0:T(1024)}, u32[]{:S(2)}) copy-start(s32[3072]{0:T(1024)} %param.9) | copy-start | bytes 36868
  7.2 200.8 %copy-start.2 = (bf16[32,1536]{1,0:T(8,128)(2,1)S(1)}, bf16[32,1536]{1,0:T(8,128)(2,1)}, u32[]{:S(2)}) copy-start(bf16[32,1536]{1,0:T(8,128)(2,1)} %param.7) | copy-start | bytes 294916
  7.2 263.9 %all-to-all-start = ((s32[16,32,3072]{2,1,0:T(8,128)}), s32[16,32,3072]{2,1,0:T(8,128)}, u32[]{:S(2)}, u32[]{:S(2)}) async-start(s32[16,32,3072]{2,1,0:T(8,128)} %bitcast.31), calls=%async_computation | async-start | bytes 12582912 | tf_op jit(solution)/shard_map/all_to_all | solution.py:53
  13.6 263.7 %all-gather.3.cloned.1.call-start = ((), (), s32[]{:S(2)}) async-start(), calls=%async_computation.1 | async-start | bytes 3244032 | tf_op jit(solution)/shard_map/all_gather | solution.py:55
  507.9 5.8 %copy-start = (f32[32,64,8,33]{1,2,3,0:T(8,128)S(1)}, f32[32,64,8,33]{1,2,3,0:T(8,128)}, u32[]{:S(2)}) copy-start(f32[32,64,8,33]{1,2,3,0:T(8,128)} %copy.38) | copy-start | bytes 6488068
  514.1 2.0 copy-start.1
Sparse Core Ops, SparseCore 0:
  17.4 133.8 all-gather.2
where the time goes:
time: 570 us; the launch traced here: 568 us
  blocking collectives  298 us (52%)
  matrix products  148 us (26%)
  local copies, waits for them, and re-layouts  81.3 us (14%)
  other arithmetic  19.1 us (3%)
  between operations  14.2 us (2%)
  starting transfers between devices  6.45 us (1%)
    all_gather x1, blocking collectives, on_device(): lax.all_gather(hessian, ('row', 'feat'), axis=0, tiled=True)  193 us
    dot_general x12, matrix products, histogram_block(): jnp.einsum('fbr,mr->fbm', onehot, masked, preferred_element_type=jnp.floa...  148 us
    psum x1, blocking collectives, on_device(): node_totals = lax.psum(local_totals, ('row', 'feat'))  43.6 us
    pmax x1, blocking collectives, on_device(): best_gain = lax.pmax(jnp.max(split_gain, axis=(0, 2)), ('row', 'feat'))  42.4 us
    mul x12, local copies, waits for them, and re-layouts, masked_rows(): picked[:, None, :] * stacked[None, :, :]  25 us
    all_gather x1, blocking collectives, on_device(): node_rows = lax.all_gather(row_node, 'row', axis=0, tiled=True)  19 us
    dynamic_slice x12, local copies, waits for them, and re-layouts, add_block(): feature_block = lax.dynamic_slice_in_dim(columns, lower, row_span, 1)  12.9 us
    dynamic_slice x12, local copies, waits for them, and re-layouts, add_block(): grad_block = lax.dynamic_slice_in_dim(grad_rows, lower, row_span, 1)  11.7 us
  transfers between devices with their start and end apart: 2, of which 0 were waited for; matrix products, arithmetic and copies ran while one was open for 1% of the time, Pallas kernels for 0%

commit v1 on v0

v1 whole, which is shorter than its diff:
```python
import functools
import math

import jax
import jax.numpy as jnp
from jax import lax
from jax.experimental import pallas as pl
from jax.experimental.pallas import tpu as pltpu
from jax.sharding import PartitionSpec as P

BINS = 64
NODES = 8
GROUP = 4
CHUNKS = 4

ridge_term = 1.0


def gain_kernel(outputs_count, bins_ref, rows_ref, gain_ref, masked_ref, sums_ref):
    step = pl.program_id(0)
    features = bins_ref.shape[1]
    subs, width = rows_ref.shape[1], rows_ref.shape[3]
    group = math.gcd(features, GROUP)
    columns = group * BINS
    channels = outputs_count + 1

    for sub in range(subs):
        block = rows_ref[0, sub].astype(jnp.float32)
        nodes = block[channels : channels + 1]
        levels = lax.broadcasted_iota(jnp.int32, (NODES, 1), 0).astype(jnp.float32)
        picked = nodes == levels
        masked = jnp.concatenate(
            [jnp.where(picked, block[k : k + 1], 0.0) for k in range(channels)], 0
        )
        masked_ref[:, sub * width : (sub + 1) * width] = masked.astype(jnp.bfloat16)

    masked = masked_ref[...]
    levels = lax.broadcasted_iota(jnp.int32, (BINS, 1), 0).astype(jnp.bfloat16)
    one, zero = jnp.bfloat16(1), jnp.bfloat16(0)
    for g in range(features // group):
        below = jnp.concatenate(
            [
                jnp.where(bins_ref[0, g * group + j : g * group + j + 1, :] <= levels, one, zero)
                for j in range(group)
            ],
            0,
        )
        part = lax.dot_general(
            masked, below, (((1,), (1,)), ((), ())), preferred_element_type=jnp.float32
        )
        where = slice(g * columns, (g + 1) * columns)

        @pl.when(step == 0)
        def _():
            sums_ref[:, where] = part

        @pl.when(step > 0)
        def _():
            sums_ref[:, where] += part

    @pl.when(step == pl.num_programs(0) - 1)
    def _():
        for g in range(features // group):
            where = slice(g * columns, (g + 1) * columns)
            left2 = right2 = whole2 = 0.0
            for k in range(channels):
                left = sums_ref[k * NODES : (k + 1) * NODES, where]
                whole = sums_ref[k * NODES : (k + 1) * NODES, BINS - 1 : BINS]
                right = whole - left
                if k < outputs_count:
                    left2 = left2 + left * left
                    right2 = right2 + right * right
                    whole2 = whole2 + whole * whole
            gain_ref[:, where] = (0.5 / outputs_count) * (
                left2 / (left + ridge_term)
                + right2 / (right + ridge_term)
                - whole2 / (whole + ridge_term)
            )


def chunk_gain(bins, rows, outputs_count):
    shards, features, shard_rows = bins.shape
    subs, width = rows.shape[1], rows.shape[3]
    sums_rows = (outputs_count + 1) * NODES
    flops = 2 * sums_rows * features * BINS * shards * shard_rows
    return pl.pallas_call(
        functools.partial(gain_kernel, outputs_count),
        out_shape=jax.ShapeDtypeStruct((NODES, features * BINS), jnp.float32),
        grid=(shards,),
        in_specs=[
            pl.BlockSpec((1, features, shard_rows), lambda i: (i, 0, 0)),
            pl.BlockSpec((1, subs, rows.shape[2], width), lambda i: (i, 0, 0, 0)),
        ],
        out_specs=pl.BlockSpec((NODES, features * BINS), lambda i: (0, 0)),
        scratch_shapes=[
            pltpu.VMEM((sums_rows, shard_rows), jnp.bfloat16),
            pltpu.VMEM((sums_rows, features * BINS), jnp.float32),
        ],
        compiler_params=pltpu.CompilerParams(
            dimension_semantics=("arbitrary",), vmem_limit_bytes=32 * 1024 * 1024
        ),
        cost_estimate=pl.CostEstimate(
            flops=flops, bytes_accessed=2 * (bins.size + rows.size), transcendentals=0
        ),
        name="chunk_gain",
    )(bins, rows)


def on_device(bin_index, gradient, hessian, row_node):
    shards, subs = lax.axis_size("row"), lax.axis_size("feat")
    owned = bin_index.shape[0] // shards
    outputs_count, width = gradient.shape
    shard_rows = bin_index.shape[1]
    nodes = lax.dynamic_slice_in_dim(row_node, lax.axis_index("feat") * width, width, 0)
    mine = jnp.concatenate(
        [gradient, hessian[None], nodes[None].astype(jnp.bfloat16)], 0
    )
    rows = lax.all_gather(mine, ("row", "feat"), axis=0, tiled=False)
    rows = rows.reshape(shards, subs, outputs_count + 2, width)

    chunks = math.gcd(CHUNKS, max(owned // GROUP, 1))
    span = owned // chunks
    bins = bin_index.reshape(shards, owned, shard_rows)
    gains = []
    for c in range(chunks):
        part = bins[:, c * span : (c + 1) * span].astype(jnp.bfloat16)
        part = lax.all_to_all(part, "row", 0, 0)
        gains.append(chunk_gain(part, rows, outputs_count))
    gain = jnp.concatenate(gains, 1)
    best_gain = lax.pmax(jnp.max(gain, axis=1), ("row", "feat"))
    split_gain = gain.reshape(NODES, owned, BINS).transpose(1, 0, 2)
    return (split_gain.reshape(owned, NODES * BINS), best_gain)


def solution(mesh):
    in_specs = (P("feat", "row"), P(None, ("row", "feat")), P(("row", "feat")), P("row"))
    out_specs = (P(("feat", "row"), None), P())
    return jax.shard_map(
        on_device, mesh=mesh, in_specs=in_specs, out_specs=out_specs, check_vma=False
    )
```

time: 570 us -> 287 us (0.50)
  blocking collectives: 298 us -> 105 us
  matrix products: 148 us -> 0 us
  Pallas kernels: 0 us -> 138 us
  local copies, waits for them, and re-layouts: 81.3 us -> 11.4 us
  other arithmetic: 19.1 us -> 6.35 us
    all_gather x2 -> x0, blocking collectives: 212 us -> none  [the longest x1 193 us: on_device(): lax.all_gather(hessian, ('row', 'feat'), axis=0, tiled=True)]
    dot_general x13 -> x0, matrix products: 148 us -> none  [the longest x12 148 us: histogram_block(): jnp.einsum('fbr,mr->fbm', onehot, masked, preferred_element_type=jnp.floa...]
    pallas_call x0 -> x4, Pallas kernels: none -> 138 us  [chunk_gain(): pl.pallas_call(functools.partial(gain_kernel, outputs_count), out_shape=j...]
    all_to_all x0 -> x2, blocking collectives: none -> 63.6 us  [on_device(): part = lax.all_to_all(part, 'row', 0, 0)]
    psum x1 -> x0, blocking collectives: 43.6 us -> none  [on_device(): node_totals = lax.psum(local_totals, ('row', 'feat'))]
    mul x12 -> x0, local copies, waits for them, and re-layouts: 25 us -> none  [masked_rows(): picked[:, None, :] * stacked[None, :, :]]
    dynamic_slice x49 -> x0, local copies, waits for them, and re-layouts: 24.8 us -> none  [the longest x12 12.9 us: add_block(): feature_block = lax.dynamic_slice_in_dim(columns, lower, row_span, 1)]
    another operation x2 -> x0, local copies, waits for them, and re-layouts: 15 us -> none  [the longest x1 7.94 us: score_splits(): left_sums = jnp.cumsum(histogram, axis=1)]
  transfers between devices with their start and end apart: 2 -> 3, of which waited for: 0 -> 0; matrix products, arithmetic and copies ran while one was open for 1% -> 2% of each run, Pallas kernels for 0% -> 36%
where the time goes in v1:
time: 287 us; the launch traced here: 286 us
  Pallas kernels  138 us (48%)
  blocking collectives  105 us (37%)
  between operations  14.1 us (5%)
  starting transfers between devices  11.7 us (4%)
  local copies, waits for them, and re-layouts  11.4 us (4%)
  other arithmetic  6.35 us (2%)
    pallas_call x4, Pallas kernels, chunk_gain(): pl.pallas_call(functools.partial(gain_kernel, outputs_count), out_shape=j...  138 us
    all_to_all x2, blocking collectives, on_device(): part = lax.all_to_all(part, 'row', 0, 0)  63.6 us
    pmax x1, blocking collectives, on_device(): best_gain = lax.pmax(jnp.max(gain, axis=1), ('row', 'feat'))  41.1 us
    all_to_all x2, starting transfers between devices, on_device(): part = lax.all_to_all(part, 'row', 0, 0)  11.6 us
    unnamed x8, local copies, waits for them, and re-layouts  8.44 us
  transfers between devices with their start and end apart: 3, of which 0 were waited for; matrix products, arithmetic and copies ran while one was open for 2% of the time, Pallas kernels for 36%

profile of v1, /device:TPU:12, one launch (start us, length us, event | category | flops | bytes accessed | tf_op | source)
XLA Modules:
  0.0 286.0 jit_solution(17822475699953308294)
XLA Ops:
  7.2 0.8 dynamic-slice_convert_fusion
  8.0 0.7 broadcast_in_dim.4
  8.7 1.6 maximum_bitcast_fusion
  10.3 3.5 %convert.7 = bf16[512,3072]{1,0:T(8,128)(2,1)S(1)} convert(s32[512,3072]{1,0:T(8,128)} %param.4) | non-fusion elementwise | flops 1572864 | bytes 9437184 | tf_op jit(solution)/shard_map/convert.3
  13.8 1.4 fusion
  15.2 28.8 %all_to_all.20.bins_ref = bf16[16,8,3072]{2,1,0:T(8,128)(2,1)S(1)} all-to-all(bf16[16,8,3072]{2,1,0:T(8,128)(2,1)S(1)} %get-tuple-element.3), channel_id=1, replica_groups=mesh['row'=16,'feat'=2] {'row'}, dimensions={0} | all-to-all | bytes 1572864 | tf_op jit(solution)/shard_map/all_to_all | solution.py:127
  43.9 34.9 %all_to_all.21.bins_ref = bf16[16,8,3072]{2,1,0:T(8,128)(2,1)S(1)} all-to-all(bf16[16,8,3072]{2,1,0:T(8,128)(2,1)S(1)} %get-tuple-element.4), channel_id=1, replica_groups=mesh['row'=16,'feat'=2] {'row'}, dimensions={0} | all-to-all | bytes 1572864 | tf_op jit(solution)/shard_map/all_to_all | solution.py:127
  78.8 5.6 %all-to-all-start = ((bf16[16,8,3072]{2,1,0:T(8,128)(2,1)}), bf16[16,8,3072]{2,1,0:T(8,128)(2,1)S(1)}, u32[]{:S(2)}, u32[]{:S(2)}) async-start(bf16[16,8,3072]{2,1,0:T(8,128)(2,1)} %get-tuple-element.2), calls=%async_computation | async-start | bytes 1572864 | tf_op jit(solution)/shard_map/all_to_all | solution.py:127
  84.5 2.1 copy-done
  86.6 34.4 %chunk_gain.7 = f32[8,512]{1,0:T(8,128)S(1)} custom-call(bf16[16,8,3072]{2,1,0:T(8,128)(2,1)S(1)} %all_to_all.20.bins_ref, bf16[16,2,34,1536]{3,2,1,0:T(8,128)(2,1)S(1)} %bitcast.5), custom_call_target="tpu_custom_call" | custom-call | flops 13287555072 | bytes 4128768 | tf_op jit(solution)/shard_map/chunk_gain/pallas_call | solution.py:86
  121.0 6.0 %all-to-all-start.1 = ((bf16[16,8,3072]{2,1,0:T(8,128)(2,1)}), bf16[16,8,3072]{2,1,0:T(8,128)(2,1)S(1)}, u32[]{:S(2)}, u32[]{:S(2)}) async-start(bf16[16,8,3072]{2,1,0:T(8,128)(2,1)} %get-tuple-element.5), calls=%async_computation.1 | async-start | bytes 1572864 | tf_op jit(solution)/shard_map/all_to_all | solution.py:127
  127.1 2.1 copy-done.1
  129.2 34.4 %chunk_gain.6 = f32[8,512]{1,0:T(8,128)S(1)} custom-call(bf16[16,8,3072]{2,1,0:T(8,128)(2,1)S(1)} %all_to_all.21.bins_ref, bf16[16,2,34,1536]{3,2,1,0:T(8,128)(2,1)S(1)} %bitcast.6), custom_call_target="tpu_custom_call" | custom-call | flops 13287555072 | bytes 4128768 | tf_op jit(solution)/shard_map/chunk_gain/pallas_call | solution.py:86
  163.6 0.1 reduce_max.38
  163.7 0.1 reduce_max.29
  163.8 2.1 copy-done.2
  165.9 34.4 %chunk_gain.4 = f32[8,512]{1,0:T(8,128)S(1)} custom-call(bf16[16,8,3072]{2,1,0:T(8,128)(2,1)S(1)} %all-to-all-done.bins_ref, bf16[16,2,34,1536]{3,2,1,0:T(8,128)(2,1)S(1)} %bitcast.7), custom_call_target="tpu_custom_call" | custom-call | flops 13287555072 | bytes 4128768 | tf_op jit(solution)/shard_map/chunk_gain/pallas_call | solution.py:86
  200.4 0.1 reduce_max.23
  200.5 2.1 copy-done.3
  202.6 34.4 %chunk_gain.5 = f32[8,512]{1,0:T(8,128)S(1)} custom-call(bf16[16,8,3072]{2,1,0:T(8,128)(2,1)S(1)} %all-to-all-done.1.bins_ref, bf16[16,2,34,1536]{3,2,1,0:T(8,128)(2,1)S(1)} %bitcast.8), custom_call_target="tpu_custom_call" | custom-call | flops 13287555072 | bytes 4128768 | tf_op jit(solution)/shard_map/chunk_gain/pallas_call | solution.py:86
  237.1 0.1 reduce_max.24
  237.2 0.1 reshape.19
  237.4 0.7 reshape.20
  238.1 41.1 %pmax.7 = f32[8]{0:T(128)} all-reduce(f32[8]{0:T(128)S(1)} %maximum_maximum_fusion), channel_id=1, replica_groups=mesh['row'=16,'feat'=2] {'row','feat'}, use_global_device_ids=true, to_apply=%region_4.5 | all-reduce | flops 8 | bytes 64 | tf_op jit(solution)/shard_map/pmax | solution.py:130
  (13 shorter events, 0.2 us)
Async XLA Ops:
  7.2 77.3 %all-gather.4.cloned.1.call-start = ((), (), s32[]{:S(2)}) async-start(), calls=%async_computation.4 | async-start | bytes 4055040 | tf_op jit(solution)/shard_map/all_gather | solution.py:118
  78.8 42.2 %all-to-all-start = ((bf16[16,8,3072]{2,1,0:T(8,128)(2,1)}), bf16[16,8,3072]{2,1,0:T(8,128)(2,1)S(1)}, u32[]{:S(2)}, u32[]{:S(2)}) async-start(bf16[16,8,3072]{2,1,0:T(8,128)(2,1)} %get-tuple-element.2), calls=%async_computation | async-start | bytes 1572864 | tf_op jit(solution)/shard_map/all_to_all | solution.py:127
  84.5 2.1 copy-start
  121.0 79.5 %all-to-all-start.1 = ((bf16[16,8,3072]{2,1,0:T(8,128)(2,1)}), bf16[16,8,3072]{2,1,0:T(8,128)(2,1)S(1)}, u32[]{:S(2)}, u32[]{:S(2)}) async-start(bf16[16,8,3072]{2,1,0:T(8,128)(2,1)} %get-tuple-element.5), calls=%async_computation.1 | async-start | bytes 1572864 | tf_op jit(solution)/shard_map/all_to_all | solution.py:127
  127.0 2.1 copy-start.1
  163.8 2.1 copy-start.2
  200.5 2.1 copy-start.3
Sparse Core Ops, SparseCore 0:
  10.9 68.8 all-gather.3

commit v2 on v1

--- a/solution.py
+++ b/solution.py
@@ -11,7 +11,7 @@
 BINS = 64
 NODES = 8
 GROUP = 4
-CHUNKS = 4
+CHUNKS = 2
 
 ridge_term = 1.0
 

time: 287 us -> 281 us (0.979)
  waiting for transfers between devices: 0.03 us -> 10.8 us
  blocking collectives: 105 us -> 97.5 us
  starting transfers between devices: 11.7 us -> 7.09 us
  local copies, waits for them, and re-layouts: 11.4 us -> 7.19 us
    all_to_all x2 -> x1, blocking collectives: 63.6 us -> 50.2 us  [on_device(): part = lax.all_to_all(part, 'row', 0, 0)]
    all_gather x1, waiting for transfers between devices: 0.01 us -> 10.8 us  [on_device(): rows = lax.all_gather(mine, ('row', 'feat'), axis=0, tiled=False)]
    pmax x1, blocking collectives: 41.1 us -> 47.3 us  [on_device(): best_gain = lax.pmax(jnp.max(gain, axis=1), ('row', 'feat'))]
    all_to_all x2 -> x1, starting transfers between devices: 11.6 us -> 7.05 us  [on_device(): part = lax.all_to_all(part, 'row', 0, 0)]
    unnamed x8 -> x4, local copies, waits for them, and re-layouts: 8.44 us -> 4.22 us
    pallas_call x4 -> x2, Pallas kernels: 138 us -> 138 us  [chunk_gain(): pl.pallas_call(functools.partial(gain_kernel, outputs_count), out_shape=j...]
  transfers between devices with their start and end apart: 3 -> 2, of which waited for: 0 -> 1; matrix products, arithmetic and copies ran while one was open for 2% -> 2% of each run, Pallas kernels for 36% -> 25%
where the time goes in v2:
time: 281 us
  Pallas kernels  138 us (49%)
  blocking collectives  97.5 us (35%)
  between operations  14.1 us (5%)
  waiting for transfers between devices  10.8 us (4%)
  local copies, waits for them, and re-layouts  7.19 us (3%)
  starting transfers between devices  7.09 us (3%)
  other arithmetic  6.11 us (2%)
    pallas_call x2, Pallas kernels, chunk_gain(): pl.pallas_call(functools.partial(gain_kernel, outputs_count), out_shape=j...  138 us
    all_to_all x1, blocking collectives, on_device(): part = lax.all_to_all(part, 'row', 0, 0)  50.2 us
    pmax x1, blocking collectives, on_device(): best_gain = lax.pmax(jnp.max(gain, axis=1), ('row', 'feat'))  47.3 us
    all_gather x1, waiting for transfers between devices, on_device(): rows = lax.all_gather(mine, ('row', 'feat'), axis=0, tiled=False)  10.8 us
    all_to_all x1, starting transfers between devices, on_device(): part = lax.all_to_all(part, 'row', 0, 0)  7.05 us
  transfers between devices with their start and end apart: 2, of which 1 were waited for; matrix products, arithmetic and copies ran while one was open for 2% of the time, Pallas kernels for 25%

profile of v2, /device:TPU:12, one launch (start us, length us, event | category | flops | bytes accessed | tf_op | source)
XLA Modules:
  0.0 281.0 jit_solution(6647180913604106240)
XLA Ops:
  7.2 0.0 all-gather.4.cloned.1.call-start
  7.2 0.8 dynamic-slice_convert_fusion
  8.0 0.7 broadcast_in_dim.4
  8.7 1.6 maximum_bitcast_fusion
  10.3 0.0 all-gather.4.cloned.1.call-update
  10.3 3.5 %convert.5 = bf16[512,3072]{1,0:T(8,128)(2,1)S(1)} convert(s32[512,3072]{1,0:T(8,128)} %param.4) | non-fusion elementwise | flops 1572864 | bytes 9437184 | tf_op jit(solution)/shard_map/convert.1
  13.8 1.4 fusion
  15.2 50.2 %all_to_all.10.bins_ref = bf16[16,16,3072]{2,1,0:T(8,128)(2,1)S(1)} all-to-all(bf16[16,16,3072]{2,1,0:T(8,128)(2,1)S(1)} %get-tuple-element.3), channel_id=1, replica_groups=mesh['row'=16,'feat'=2] {'row'}, dimensions={0} | all-to-all | bytes 3145728 | tf_op jit(solution)/shard_map/all_to_all | solution.py:127
  65.4 7.1 %all-to-all-start = ((bf16[16,16,3072]{2,1,0:T(8,128)(2,1)}), bf16[16,16,3072]{2,1,0:T(8,128)(2,1)S(1)}, u32[]{:S(2)}, u32[]{:S(2)}) async-start(bf16[16,16,3072]{2,1,0:T(8,128)(2,1)} %get-tuple-element.2), calls=%async_computation | async-start | bytes 3145728 | tf_op jit(solution)/shard_map/all_to_all | solution.py:127
  72.5 10.8 %all-gather.4.cloned.1.call-done = bf16[32,34,1536]{2,1,0:T(8,128)(2,1)} async-done(((bf16[1,34,1536]{2,1,0:T(8,128)(2,1)}), bf16[32,34,1536]{2,1,0:T(8,128)(2,1)}) %all-gather.4.cloned.1.call-update) | async-done | bytes 3342352 | tf_op jit(solution)/shard_map/all_gather | solution.py:118
  83.2 0.0 copy-start
  83.2 2.1 copy-done
  85.3 69.1 %chunk_gain.3 = f32[8,1024]{1,0:T(8,128)S(1)} custom-call(bf16[16,16,3072]{2,1,0:T(8,128)(2,1)S(1)} %all_to_all.10.bins_ref, bf16[16,2,34,1536]{3,2,1,0:T(8,128)(2,1)S(1)} %bitcast.5), custom_call_target="tpu_custom_call" | custom-call | flops 26575110144 | bytes 4915200 | tf_op jit(solution)/shard_map/chunk_gain/pallas_call | solution.py:86
  154.4 0.0 all-to-all-done.bins_ref
  154.4 0.0 copy-start.1
  154.5 2.1 copy-done.1
  156.6 69.1 %chunk_gain.2 = f32[8,1024]{1,0:T(8,128)S(1)} custom-call(bf16[16,16,3072]{2,1,0:T(8,128)(2,1)S(1)} %all-to-all-done.bins_ref, bf16[16,2,34,1536]{3,2,1,0:T(8,128)(2,1)S(1)} %bitcast.6), custom_call_target="tpu_custom_call" | custom-call | flops 26575110144 | bytes 4915200 | tf_op jit(solution)/shard_map/chunk_gain/pallas_call | solution.py:86
  225.7 0.1 reduce_max.14
  225.8 0.1 reduce_max.18
  225.9 0.1 reshape.19
  226.0 0.1 copy.7
  226.1 0.7 reshape.20
  226.8 47.3 %pmax.7 = f32[8]{0:T(128)} all-reduce(f32[8]{0:T(128)S(1)} %reduce_max.19), channel_id=1, replica_groups=mesh['row'=16,'feat'=2] {'row','feat'}, use_global_device_ids=true, to_apply=%region_2.3 | all-reduce | flops 8 | bytes 64 | tf_op jit(solution)/shard_map/pmax | solution.py:130
  (3 shorter events, 0.0 us)
Async XLA Ops:
  7.2 76.1 %all-gather.4.cloned.1.call-start = ((), (), s32[]{:S(2)}) async-start(), calls=%async_computation.2 | async-start | bytes 4055040 | tf_op jit(solution)/shard_map/all_gather | solution.py:118
  65.4 89.0 %all-to-all-start = ((bf16[16,16,3072]{2,1,0:T(8,128)(2,1)}), bf16[16,16,3072]{2,1,0:T(8,128)(2,1)S(1)}, u32[]{:S(2)}, u32[]{:S(2)}) async-start(bf16[16,16,3072]{2,1,0:T(8,128)(2,1)} %get-tuple-element.2), calls=%async_computation | async-start | bytes 3145728 | tf_op jit(solution)/shard_map/all_to_all | solution.py:127
  83.2 2.1 copy-start
  154.4 2.1 copy-start.1
Sparse Core Ops, SparseCore 0:
  10.9 72.2 all-gather.3
